TPU v7x, 32 devices: a whole 2x2x4 slice. The times are simulated.
32 devices in a mesh: client: 4 (over z), tensor: 4 (over x, core), sdata: 2 (over y).
Axes of the slice: x: 2, y: 2, z: 4, core: 2. Of those that a mesh axis runs over, the one named last changes fastest.
Arguments:
- client_input: bfloat16 [3072, 2048], P(('client', 'sdata')), may hold values from -6 to 6
- client_gain: bfloat16 [4, 2048], P('client'), may hold values from 0.5 to 1.5
- query_weight: bfloat16 [4, 2048, 2048], P('client', None, 'tensor'), as said below
- key_weight: bfloat16 [4, 2048, 512], P('client', None, 'tensor'), as said below
- client_value_weight: bfloat16 [4, 2048, 512], P('client', None, 'tensor'), may hold values from -0.125 to 0.125
- output_weight: bfloat16 [4, 2048, 2048], P('client', None, 'tensor'), may hold values from -0.125 to 0.125
- server_gain: bfloat16 [2, 2048], P('sdata'), may hold values from 0.5 to 1.5
- server_gate: bfloat16 [2, 2048, 4096], P('sdata', None, 'tensor'), may hold values from -0.125 to 0.125
- server_up: bfloat16 [2, 2048, 4096], P('sdata', None, 'tensor'), may hold values from -0.125 to 0.125
- server_down: bfloat16 [2, 4096, 2048], P('sdata', 'tensor'), may hold values from -0.09375 to 0.09375
- upstream: bfloat16 [3072, 2048], P(('client', 'sdata')), may hold values from -6 to 6
- assignment: int32 [4], replicated, may hold values from 0 to 1, as said below
Outputs:
- query_update: bfloat16 [2048, 2048], P(('client', 'sdata'), 'tensor')
- key_update: bfloat16 [2048, 512], P(('client', 'sdata'), 'tensor')
- value_update: bfloat16 [2048, 512], P(('client', 'sdata'), 'tensor')
- output_update: bfloat16 [2048, 2048], P(('client', 'sdata'), 'tensor')
Inputs may be any that keep to these rules, and one draw needn't show every extreme that they name: `assignment`: each of the 2 server groups is named by exactly 2 clients. `query_weight`: independent entries with a spread of about 2048 ** -0.5. `key_weight`: entries with a spread of about 2048 ** -0.5 or more.
All inputs are finite; a program needn't handle non-finite values.
Results may differ from a plain program's by a relative error of at most 0.038.
The roundings to bfloat16 on the way count: a program that leaves them out, or rounds other values in their place, can miss the bound.
Values may be sent and summed in bfloat16 or wider, within the bound.
A program may use at most 128 MiB of HBM per device.

v0:
```python
from functools import partial
import math

import jax
import jax.numpy as jnp
from jax import lax
from jax.sharding import PartitionSpec as P

HEAD_DIM = 64


def rotary_tables(length):
    halfway = HEAD_DIM // 2
    positions = jnp.arange(length).astype(jnp.float32)
    exponents = jnp.arange(halfway).astype(jnp.float32) * (2.0 / HEAD_DIM)
    frequencies = jnp.exp(-math.log(500000.0) * exponents)
    angles = positions[:, None] * frequencies[None, :]
    cosine_table = jnp.concatenate([jnp.cos(angles), jnp.cos(angles)], 1)
    sine_table = jnp.concatenate([jnp.sin(angles), jnp.sin(angles)], 1)
    return (cosine_table, sine_table)


def rotary(heads_in, cosine_table, sine_table):
    halfway = heads_in.shape[-1] // 2
    turned = jnp.concatenate([-heads_in[..., halfway:], heads_in[..., :halfway]], -1)
    return heads_in * cosine_table[:, None, :] + turned * sine_table[:, None, :]


def normalize(rows_in, gain):
    rows_float = rows_in.astype(jnp.float32)
    inv_rms = lax.rsqrt(jnp.mean(rows_float * rows_float, -1, keepdims=True) + 1e-05)
    return (rows_float * inv_rms * gain.astype(jnp.float32)).astype(jnp.bfloat16)


def attention_part(normed, query_matrix, client_key_matrix, value_matrix, output_matrix):
    length = normed.shape[0]
    query_count = query_matrix.shape[1] // HEAD_DIM
    shared_count = client_key_matrix.shape[1] // HEAD_DIM
    group_size = query_count // shared_count
    cosine_table, sine_table = rotary_tables(length)
    queries = jnp.dot(normed, query_matrix, preferred_element_type=jnp.float32).reshape(
        length, query_count, HEAD_DIM
    )
    queries = (
        rotary(queries, cosine_table, sine_table)
        .astype(jnp.bfloat16)
        .reshape(length, shared_count, group_size, HEAD_DIM)
    )
    key_heads = jnp.dot(normed, client_key_matrix, preferred_element_type=jnp.float32).reshape(
        length, shared_count, HEAD_DIM
    )
    key_heads = rotary(key_heads, cosine_table, sine_table).astype(jnp.bfloat16)
    value_heads = (
        jnp.dot(normed, value_matrix, preferred_element_type=jnp.float32)
        .astype(jnp.bfloat16)
        .reshape(length, shared_count, HEAD_DIM)
    )
    scores = jnp.einsum(
        "qgrd,kgd->grqk", queries.astype(jnp.float32), key_heads.astype(jnp.float32)
    ) * HEAD_DIM ** (-0.5)
    row_ids = lax.broadcasted_iota(jnp.int32, (length, length), 0)
    col_ids = lax.broadcasted_iota(jnp.int32, (length, length), 1)
    scores = jnp.where(col_ids <= row_ids, scores, -1e30)
    highest = lax.stop_gradient(jnp.max(scores, -1, keepdims=True))
    exponent = jnp.exp(scores - highest)
    weights = (exponent / jnp.sum(exponent, -1, keepdims=True)).astype(jnp.bfloat16)
    context = jnp.einsum(
        "grqk,kgd->qgrd", weights.astype(jnp.float32), value_heads.astype(jnp.float32)
    )
    context = context.astype(jnp.bfloat16).reshape(length, query_count * HEAD_DIM)
    return lax.dot_general(
        context, output_matrix, (((1,), (1,)), ((), ())), preferred_element_type=jnp.float32
    )


def server_pull(rows_in, upstream_rows, gain, gate_matrix, up_matrix, down_matrix):
    rows_float = rows_in.astype(jnp.float32)
    inv_rms = lax.rsqrt(jnp.mean(rows_float * rows_float, -1, keepdims=True) + 1e-05)
    gain_float = gain.astype(jnp.float32)
    server_normed = (rows_float * inv_rms * gain_float).astype(jnp.bfloat16)
    gate_value = jnp.dot(server_normed, gate_matrix, preferred_element_type=jnp.float32)
    up_value = jnp.dot(server_normed, up_matrix, preferred_element_type=jnp.float32)
    pulled = lax.dot_general(
        upstream_rows, down_matrix, (((1,), (1,)), ((), ())), preferred_element_type=jnp.float32
    )
    sigmoid_gate = jax.nn.sigmoid(gate_value)
    gate_grad = (
        pulled * up_value * sigmoid_gate * (1.0 + gate_value * (1.0 - sigmoid_gate))
    ).astype(jnp.bfloat16)
    up_grad = (pulled * gate_value * sigmoid_gate).astype(jnp.bfloat16)
    normed_grad = lax.dot_general(
        gate_grad, gate_matrix, (((1,), (1,)), ((), ())), preferred_element_type=jnp.float32
    )
    normed_grad = normed_grad + lax.dot_general(
        up_grad, up_matrix, (((1,), (1,)), ((), ())), preferred_element_type=jnp.float32
    )
    weighted = normed_grad * gain_float
    return inv_rms * weighted - rows_float * inv_rms**3 * jnp.mean(
        weighted * rows_float, -1, keepdims=True
    )


def over_clients(pieces):
    return lax.all_to_all(pieces, "client", split_axis=1, concat_axis=1, tiled=True)


def over_groups(pieces):
    return lax.all_to_all(pieces, "sdata", split_axis=1, concat_axis=1, tiled=True)


def relay_out(stacked, group_order, client_count):
    count_rows, length, breadth = stacked.shape
    pieces = stacked.reshape(count_rows, client_count, length // client_count, breadth)
    arrived = jnp.take(over_clients(pieces), group_order, axis=1)
    return over_groups(arrived).reshape(count_rows, length, breadth)


def relay_back(stacked, inverse, client_count):
    count_rows, length, breadth = stacked.shape
    pieces = stacked.reshape(count_rows, client_count, length // client_count, breadth)
    arrived = jnp.take(over_groups(pieces), inverse, axis=1)
    return over_clients(arrived).reshape(count_rows, length, breadth)


def share_sum(partial_rows):
    return lax.psum_scatter(
        partial_rows.astype(jnp.bfloat16), "tensor", scatter_dimension=1, tiled=True
    ).astype(jnp.float32)


def widen_rows(stacked):
    return lax.all_gather(stacked, "tensor", axis=2, tiled=True)


def local(
    client_input,
    client_gain,
    query_weight,
    key_weight,
    client_value_weight,
    output_weight,
    server_gain,
    server_gate,
    server_up,
    server_down,
    upstream,
    assignment,
):
    client_count = lax.axis_size("client")
    normed = normalize(client_input, client_gain[0])
    attended, pullback = jax.vjp(
        partial(attention_part, normed),
        query_weight[0],
        key_weight[0],
        client_value_weight[0],
        output_weight[0],
    )
    group_order = jnp.argsort(assignment, stable=True)
    inverse = jnp.argsort(group_order, stable=True)
    shard_width = client_input.shape[1] // lax.axis_size("tensor")
    shard_start = lax.axis_index("tensor") * shard_width
    own_input = lax.dynamic_slice_in_dim(client_input, shard_start, shard_width, 1)
    own_upstream = lax.dynamic_slice_in_dim(upstream, shard_start, shard_width, 1)
    cut_input = (own_input.astype(jnp.float32) + share_sum(attended)).astype(jnp.bfloat16)
    arrived = relay_out(jnp.stack([cut_input, own_upstream]), group_order, client_count)
    widened = widen_rows(arrived)
    pulled = server_pull(
        widened[0], widened[1], server_gain[0], server_gate[0], server_up[0], server_down[0]
    )
    cut_grad = (share_sum(pulled) + arrived[1].astype(jnp.float32)).astype(jnp.bfloat16)
    returned = relay_back(cut_grad[None], inverse, client_count)
    arriving_grad = widen_rows(returned)[0]
    query_grad, key_grad, value_grad, output_grad = pullback(arriving_grad.astype(jnp.float32))
    query_width = query_grad.shape[1]
    key_width = key_grad.shape[1]
    joined_grads = jnp.concatenate(
        [
            query_grad.astype(jnp.float32),
            key_grad.astype(jnp.float32),
            value_grad.astype(jnp.float32),
            output_grad.astype(jnp.float32),
        ],
        1,
    )
    summed = (
        lax.psum_scatter(
            joined_grads.astype(jnp.bfloat16), ("client", "sdata"), scatter_dimension=0, tiled=True
        ).astype(jnp.float32)
        / client_count
    )
    query_update = summed[:, :query_width].astype(jnp.bfloat16)
    key_update = summed[:, query_width : query_width + key_width].astype(jnp.bfloat16)
    value_update = summed[:, query_width + key_width : query_width + 2 * key_width].astype(
        jnp.bfloat16
    )
    output_update = summed[:, query_width + 2 * key_width :].astype(jnp.bfloat16)
    return (query_update, key_update, value_update, output_update)


def solution(mesh):
    placed = (
        P(("client", "sdata"), None),
        P("client", None),
        P("client", None, "tensor"),
        P("client", None, "tensor"),
        P("client", None, "tensor"),
        P("client", None, "tensor"),
        P("sdata", None),
        P("sdata", None, "tensor"),
        P("sdata", None, "tensor"),
        P("sdata", "tensor", None),
        P(("client", "sdata"), None),
        P(),
    )
    return jax.shard_map(
        local,
        mesh=mesh,
        in_specs=placed,
        out_specs=(
            P(("client", "sdata"), "tensor"),
            P(("client", "sdata"), "tensor"),
            P(("client", "sdata"), "tensor"),
            P(("client", "sdata"), "tensor"),
        ),
        check_vma=False,
    )
```

profile of v0, /device:TPU:8, one launch (start us, length us, event | category | flops | bytes accessed | tf_op | source)
XLA Modules:
  0.0 375.5 jit_solution(15305988883299019930)
XLA Ops:
  7.3 1.9 fusion.21
  10.0 1.2 copy.36
  11.2 2.4 convolution_convert_fusion.8
  14.3 4.0 %copy.37 = bf16[1,2048,512]{1,2,0:T(8,128)(2,1)} copy(bf16[1,2048,512]{2,1,0:T(8,128)(2,1)} %param.14) | data formatting | bytes 4194304 | tf_op args[2]
  18.3 3.4 fusion.40
  22.7 0.9 fusion.7
  23.6 1.0 fusion.33
  24.6 1.1 divide_convert_fusion
  25.8 1.5 copy-done.2
  28.6 2.2 convolution_convert_fusion.2
  30.9 1.0 constant_dynamic-slice_fusion
  31.9 28.3 %reduce-scatter.4.cloned.1.call-done = bf16[384,512]{1,0:T(8,128)(2,1)} async-done(((bf16[384,2048]{1,0:T(8,128)(2,1)}), bf16[384,512]{1,0:T(8,128)(2,1)}) %reduce-scatter.4.cloned.1.call-update) | async-done | bytes 393232 | tf_op jit(solution)/shard_map/reduce_scatter | solution.py:126
  60.2 1.2 add_convert_fusion
  61.4 1.0 pad_maximum_fusion.1
  62.4 5.1 %all-to-all-start = ((bf16[2,4,96,512]{3,2,0,1:T(8,128)(2,1)}), bf16[2,4,96,512]{3,2,0,1:T(8,128)(2,1)S(1)}, u32[]{:S(2)}, u32[]{:S(2)}) async-start(bf16[2,4,96,512]{3,2,0,1:T(8,128)(2,1)} %pad_maximum_fusion.1), calls=%async_computation.1 | async-start | bytes 1572864 | tf_op jit(solution)/shard_map/all_to_all | solution.py:104
  68.1 1.4 sort.31
  70.0 14.2 %all-to-all-done = bf16[2,4,96,512]{3,2,0,1:T(8,128)(2,1)S(1)} async-done(((bf16[2,4,96,512]{3,2,0,1:T(8,128)(2,1)}), bf16[2,4,96,512]{3,2,0,1:T(8,128)(2,1)S(1)}, u32[]{:S(2)}, u32[]{:S(2)}) %all-to-all-start) | async-done | bytes 786464 | tf_op jit(solution)/shard_map/all_to_all | solution.py:104
  84.2 1.5 gather_fusion
  85.8 1.3 select_bitcast_fusion
  87.1 12.2 %all_to_all.20 = bf16[2,4,96,512]{3,2,0,1:T(8,128)(2,1)S(1)} all-to-all(bf16[2,4,96,512]{3,2,0,1:T(8,128)(2,1)S(1)} %select_bitcast_fusion), channel_id=1, replica_groups=mesh['client'=4,'tensor'=4,'sdata'=2] {'sdata'}, dimensions={1} | all-to-all | bytes 1572864 | tf_op jit(solution)/shard_map/all_to_all | solution.py:108
  99.3 1.0 copy.40
  101.2 27.8 %all-gather.3.cloned.1.call-done = bf16[2,384,2048]{2,1,0:T(8,128)(2,1)} async-done(((bf16[2,384,512]{2,1,0:T(8,128)(2,1)}), bf16[2,384,2048]{2,1,0:T(8,128)(2,1)}) %all-gather.3.cloned.1.call-update) | async-done | bytes 3145744 | tf_op jit(solution)/shard_map/all_gather | solution.py:132
  128.9 1.8 fusion.24
  130.8 5.8 %fusion.16 = f32[384,1024]{1,0:T(8,128)} fusion(bf16[1,1024,2048]{2,1,0:T(8,128)(2,1)} %param.21, bf16[2,384,2048]{2,1,0:T(8,128)(2,1)} %all-gather.3.cloned.1.call-done), kind=kOutput, calls=%fused_computation.24 | convolution fusion | flops 1610612736 | bytes 7340032 | tf_op jit(solution)/shard_map/dot_general | solution.py:83
  136.6 3.0 fusion.10
  139.6 10.2 %fusion.8 = f32[384,2048]{1,0:T(8,128)} fusion(bf16[1,2048,1024]{2,1,0:T(8,128)(2,1)} %param.19, f32[384,1024]{1,0:T(8,128)} %fusion.10, f32[384,1024]{1,0:T(8,128)} %fusion.16, bf16[1,2048,1024]{2,1,0:T(8,128)(2,1)} %param.20, f32[2048]{0:T(1024)} %bitcast.225, f32[384]{0:T(512)S(1)} %get-tuple-element.35, ...), kind=kOutput, calls=%fused_computation.16 | convolution fusion | flops 3228303360 | bytes 16262656 | tf_op jit(solution)/shard_map/dot_general | solution.py:91
  149.9 6.8 %fusion.28 = (f32[384]{0:T(512)S(1)}, f32[384,2048]{1,0:T(8,128)S(1)}) fusion(bf16[2,384,2048]{2,1,0:T(8,128)(2,1)} %all-gather.3.cloned.1.call-done, f32[2048]{0:T(1024)} %bitcast.226, f32[384,2048]{1,0:T(8,128)} %fusion.8, bf16[1,2048,1024]{2,1,0:T(8,128)(2,1)} %param.20, f32[384,1024]{1,0:T(8,128)} %fusion.16, f32[384,1024]{1,0:T(8,128)} %fusion.10), kind=kOutput, calls=%fused_computation.40 | convolution fusion | flops 1616903808 | bytes 15214080 | tf_op jit(solution)/shard_map/dot_general | solution.py:94
  156.7 1.9 fusion.27
  158.6 1.4 sort.32
  161.3 25.4 %reduce-scatter.6.cloned.1.call-done = bf16[384,512]{1,0:T(8,128)(2,1)} async-done(((bf16[384,2048]{1,0:T(8,128)(2,1)}), bf16[384,512]{1,0:T(8,128)(2,1)}) %reduce-scatter.6.cloned.1.call-update) | async-done | bytes 393232 | tf_op jit(solution)/shard_map/reduce_scatter | solution.py:126
  186.7 1.9 fusion.59
  188.7 3.5 all-to-all-start.2
  192.8 6.0 %all-to-all-done.2 = bf16[1,4,96,512]{3,2,0,1:T(8,128)(2,1)S(1)} async-done(((bf16[1,4,96,512]{3,2,0,1:T(8,128)(2,1)}), bf16[1,4,96,512]{3,2,0,1:T(8,128)(2,1)S(1)}, u32[]{:S(2)}, u32[]{:S(2)}) %all-to-all-start.2) | async-done | bytes 393248 | tf_op jit(solution)/shard_map/all_to_all | solution.py:108
  199.5 13.9 %all_to_all.21 = bf16[1,4,96,512]{3,2,0,1:T(8,128)(2,1)} all-to-all(bf16[1,4,96,512]{3,2,0,1:T(8,128)(2,1)S(1)} %fusion.65), channel_id=1, replica_groups=mesh['client'=4,'tensor'=4,'sdata'=2] {'client'}, dimensions={1} | all-to-all | bytes 786432 | tf_op jit(solution)/shard_map/all_to_all | solution.py:104
  213.8 17.9 %all-gather.5.cloned.1.call-done = bf16[1,384,2048]{2,1,0:T(8,128)(2,1)} async-done(((bf16[1,384,512]{2,1,0:T(8,128)(2,1)}), bf16[1,384,2048]{2,1,0:T(8,128)(2,1)}) %all-gather.5.cloned.1.call-update) | async-done | bytes 1572880 | tf_op jit(solution)/shard_map/all_gather | solution.py:132
  231.7 3.1 fusion.46
  234.9 1.2 copy.43
  236.1 2.6 fusion.54
  238.8 4.0 %fusion.6 = (f32[2,4,384]{2,1,0:T(4,128)S(1)}, bf16[2,4,384,384]{2,3,1,0:T(8,128)(2,1)S(1)}) fusion(f32[2,384,384,4]{2,1,3,0:T(8,128)} %copy-done.1, f32[2,4,384]{2,1,0:T(4,128)S(1)} %multiply_divide_fusion, f32[2,4,384]{2,1,0:T(4,128)S(1)} %get-tuple-element.36, pred[384,384]{0,1:T(8,128)(4,1)S(1)} %iota_compare_fusion, ...), kind=kOutput, calls=%fused_computation.11 | convolution fusion | flops 160429056 | bytes 7753728 | tf_op jit(solution)/shard_map/transpose(jvp(grqk,kgd->qgrd))/dot_general | solution.py:67
  242.9 1.9 fusion.4
  244.8 0.8 fusion.53
  248.0 1.4 convolution_convert_fusion.1
  249.5 1.3 convolution_convert_fusion
  250.8 10.1 %pad_maximum_fusion = bf16[2048,1280]{0,1:T(8,128)(2,1)} fusion(bf16[2048,512]{0,1:T(8,128)(2,1)S(1)} %convolution_convert_fusion, bf16[2048,128]{0,1:T(8,128)(2,1)S(1)} %convolution_convert_fusion.3, bf16[2048,128]{0,1:T(8,128)(2,1)S(1)} %convolution_convert_fusion.4, bf16[2048,512]{0,1:T(8,128)(2,1)S(1)} %convolution_convert_fusion.1), kind=kLoop, calls=%fused_computation.4 | loop fusion | flops 20971520 | bytes 10485760 | tf_op jit(solution)/shard_map/concatenate | solution.py:176
  260.9 103.6 %reduce-scatter.8.cloned.1.call-done = bf16[256,1280]{0,1:T(8,128)(2,1)} async-done(((bf16[2048,1280]{0,1:T(8,128)(2,1)}), bf16[256,1280]{0,1:T(8,128)(2,1)}) %reduce-scatter.8.cloned.1.call-update) | async-done | bytes 655376 | tf_op jit(solution)/shard_map/reduce_scatter | solution.py:186
  364.5 1.2 multiply_convert_fusion.2
  365.8 0.8 copy.48
  368.1 0.8 copy.45
  (109 shorter events, 12.7 us)
Async XLA Ops:
  7.2 21.4 %copy-start = (bf16[1,2048,512]{2,1,0:T(8,128)(2,1)S(1)}, bf16[1,2048,512]{2,1,0:T(8,128)(2,1)}, u32[]{:S(2)}) copy-start(bf16[1,2048,512]{2,1,0:T(8,128)(2,1)} %param.17) | copy-start | bytes 6291460
  7.2 53.0 %reduce-scatter.4.cloned.1.call-start = ((), (), s32[]{:S(2)}) async-start(), calls=%async_computation.7 | async-start | bytes 1966080 | tf_op jit(solution)/shard_map/reduce_scatter | solution.py:126
  9.2 9.1 %copy-start.19 = (f32[384]{0:T(512)}, f32[384]{0:T(512)S(1)}, u32[]{:S(2)}) copy-start(f32[384]{0:T(512)S(1)} %add_rsqrt_fusion.1) | copy-start | bytes 4612
  9.9 8.3 %copy-start.16 = (f32[1,2048]{1,0:T(1,128)}, f32[1,2048]{1,0:T(1,128)S(1)}, u32[]{:S(2)}) copy-start(f32[1,2048]{1,0:T(1,128)S(1)} %mul.315) | copy-start | bytes 24580
  11.2 2.4 copy-start.7
  13.6 12.2 %copy-start.13 = (bf16[384,128]{0,1:T(8,128)(2,1)}, bf16[384,128]{0,1:T(8,128)(2,1)S(1)}, u32[]{:S(2)}) copy-start(bf16[384,128]{0,1:T(8,128)(2,1)S(1)} %convolution_convert_fusion.8) | copy-start | bytes 294916
  22.1 0.6 copy-start.5
  22.1 1.5 copy-start.9
  23.6 2.2 copy-start.1
  25.8 1.5 copy-start.2
  27.8 0.8 copy-start.11
  30.8 37.2 %copy-start.23 = (s32[4]{0:T(128)S(1)}, s32[4]{0:T(128)}, u32[]{:S(2)}) copy-start(s32[4]{0:T(128)} %param.23) | copy-start | bytes 52
  62.4 21.8 %all-to-all-start = ((bf16[2,4,96,512]{3,2,0,1:T(8,128)(2,1)}), bf16[2,4,96,512]{3,2,0,1:T(8,128)(2,1)S(1)}, u32[]{:S(2)}, u32[]{:S(2)}) async-start(bf16[2,4,96,512]{3,2,0,1:T(8,128)(2,1)} %pad_maximum_fusion.1), calls=%async_computation.1 | async-start | bytes 1572864 | tf_op jit(solution)/shard_map/all_to_all | solution.py:104
  67.6 61.4 %all-gather.3.cloned.1.call-start = ((), (), s32[]{:S(2)}) async-start(), calls=%async_computation.8 | async-start | bytes 3932160 | tf_op jit(solution)/shard_map/all_gather | solution.py:132
  69.5 14.8 %copy-start.24 = (s32[4]{0:T(128)}, s32[4]{0:T(128)S(1)}, u32[]{:S(2)}) copy-start(s32[4]{0:T(128)S(1)} %get-tuple-element.6) | copy-start | bytes 52
  85.8 14.8 %copy-start.15 = (bf16[1,2048]{1,0:T(2,128)(2,1)S(1)}, bf16[1,2048]{1,0:T(2,128)(2,1)}, u32[]{:S(2)}) copy-start(bf16[1,2048]{1,0:T(2,128)(2,1)} %param.18) | copy-start | bytes 12292
  100.3 86.4 %reduce-scatter.6.cloned.1.call-start = ((), (), s32[]{:S(2)}) async-start(), calls=%async_computation.9 | async-start | bytes 1966080 | tf_op jit(solution)/shard_map/reduce_scatter | solution.py:126
  130.8 5.8 %copy-start.3 = (bf16[2,384,2048]{2,1,0:T(8,128)(2,1)S(1)}, bf16[2,384,2048]{2,1,0:T(8,128)(2,1)}, u32[]{:S(2)}) copy-start(bf16[2,384,2048]{2,1,0:T(8,128)(2,1)} %all-gather.3.cloned.1.call-done) | copy-start | bytes 9437188
  130.8 5.8 %copy-start.18 = (f32[1,2048]{1,0:T(1,128)S(1)}, f32[1,2048]{1,0:T(1,128)}, u32[]{:S(2)}) copy-start(f32[1,2048]{1,0:T(1,128)} %mul.316) | copy-start | bytes 24580
  130.8 5.8 %copy-start.21 = (bf16[1,2048,1024]{2,1,0:T(8,128)(2,1)S(1)}, bf16[1,2048,1024]{2,1,0:T(8,128)(2,1)}, u32[]{:S(2)}) copy-start(bf16[1,2048,1024]{2,1,0:T(8,128)(2,1)} %param.19) | copy-start | bytes 12582916
  149.9 6.8 %copy-start.4 = (bf16[2,384,2048]{2,1,0:T(8,128)(2,1)S(1)}, bf16[2,384,2048]{2,1,0:T(8,128)(2,1)}, u32[]{:S(2)}) copy-start(bf16[2,384,2048]{2,1,0:T(8,128)(2,1)} %all-gather.3.cloned.1.call-done) | copy-start | bytes 9437188
  160.0 0.5 copy-start.25
  188.7 10.2 %all-to-all-start.2 = ((bf16[1,4,96,512]{3,2,0,1:T(8,128)(2,1)}), bf16[1,4,96,512]{3,2,0,1:T(8,128)(2,1)S(1)}, u32[]{:S(2)}, u32[]{:S(2)}) async-start(bf16[1,4,96,512]{3,2,0,1:T(8,128)(2,1)} %bitcast.33), calls=%async_computation.4 | async-start | bytes 786432 | tf_op jit(solution)/shard_map/all_to_all | solution.py:108
  192.1 39.6 %all-gather.5.cloned.1.call-start = ((), (), s32[]{:S(2)}) async-start(), calls=%async_computation.10 | async-start | bytes 1966080 | tf_op jit(solution)/shard_map/all_gather | solution.py:132
  213.4 151.1 %reduce-scatter.8.cloned.1.call-start = ((), (), s32[]{:S(2)}) async-start(), calls=%async_computation.11 | async-start | bytes 5898240 | tf_op jit(solution)/shard_map/reduce_scatter | solution.py:186
  234.9 3.9 %copy-start.14 = (bf16[384,128]{0,1:T(8,128)(2,1)S(1)}, bf16[384,128]{0,1:T(8,128)(2,1)}, u32[]{:S(2)}) copy-start(bf16[384,128]{0,1:T(8,128)(2,1)} %copy-done.13) | copy-start | bytes 294916
  236.1 6.7 %slice-start = ((s8[4718592]{0:T(1024)(128)(4,1)}), s8[4194304]{0:T(1024)(128)(4,1)S(1)}, s32[]{:S(2)}) async-start(s8[4718592]{0:T(1024)(128)(4,1)} %bitcast.197), calls=%async_computation.12 | async-start | bytes 8388608
  238.8 4.1 %slice-start.1 = ((s8[4718592]{0:T(1024)(128)(4,1)}), s8[524288]{0:T(1024)(128)(4,1)S(1)}, s32[]{:S(2)}) async-start(s8[4718592]{0:T(1024)(128)(4,1)} %bitcast.197), calls=%async_computation.13 | async-start | bytes 1048576
  242.8 2.8 copy-start.10
  244.8 1.4 copy-start.8
  244.8 1.4 copy-start.17
  244.8 1.4 copy-start.20
  245.7 1.3 copy-start.6
  248.0 1.4 copy-start.12
  248.0 1.5 copy-start.22
Sparse Core Ops, SparseCore 0:
  31.0 29.1 reduce-scatter.3
  100.5 28.4 all-gather.2
  158.7 27.9 reduce-scatter.5
  213.6 18.1 all-gather.4
  261.0 103.4 reduce-scatter.7
where the time goes:
time: 378 us; the launch traced here: 375 us
  waiting for transfers between devices  223 us (59%)
  matrix products  51.1 us (14%)
  other arithmetic  32.9 us (9%)
  blocking collectives  26.1 us (7%)
  local copies, waits for them, and re-layouts  18.5 us (5%)
  between operations  14.4 us (4%)
  starting transfers between devices  9.16 us (2%)
    reduce_scatter x1, waiting for transfers between devices, local(): lax.psum_scatter(joined_grads.astype(jnp.bfloat16), ('client', 'sdata'),...  104 us
    reduce_scatter x2, waiting for transfers between devices, share_sum(): lax.psum_scatter(partial_rows.astype(jnp.bfloat16), 'tensor', scatter_dim...  53.7 us
    all_gather x2, waiting for transfers between devices, widen_rows(): return lax.all_gather(stacked, 'tensor', axis=2, tiled=True)  45.7 us
    all_to_all x1, waiting for transfers between devices, over_clients(): lax.all_to_all(pieces, 'client', split_axis=1, concat_axis=1, tiled=True)  14.2 us
    all_to_all x1, blocking collectives, over_clients(): lax.all_to_all(pieces, 'client', split_axis=1, concat_axis=1, tiled=True)  13.9 us
    all_to_all x1, blocking collectives, over_groups(): lax.all_to_all(pieces, 'sdata', split_axis=1, concat_axis=1, tiled=True)  12.2 us
    unnamed x62, local copies, waits for them, and re-layouts  11.7 us
    dot_general x1, matrix products, server_pull(): lax.dot_general(gate_grad, gate_matrix, (((1,), (1,)), ((), ())), preferr...  10.2 us
  transfers between devices with their start and end apart: 7, of which 7 were waited for; matrix products, arithmetic and copies ran while one was open for 2% of the time, Pallas kernels for 0%

commit v1 on v0

--- a/solution.py
+++ b/solution.py
@@ -4,9 +4,15 @@
 import jax
 import jax.numpy as jnp
 from jax import lax
+from jax.experimental import pallas as pl
+from jax.experimental.pallas import tpu as pltpu
 from jax.sharding import PartitionSpec as P
 
 HEAD_DIM = 64
+MESH = pl.DeviceIdType.MESH
+CORES = 2
+BF16 = jnp.bfloat16
+F32 = jnp.float32
 
 
 def rotary_tables(length):
@@ -100,36 +106,431 @@
     )
 
 
-def over_clients(pieces):
-    return lax.all_to_all(pieces, "client", split_axis=1, concat_axis=1, tiled=True)
-
-
-def over_groups(pieces):
-    return lax.all_to_all(pieces, "sdata", split_axis=1, concat_axis=1, tiled=True)
-
-
-def relay_out(stacked, group_order, client_count):
-    count_rows, length, breadth = stacked.shape
-    pieces = stacked.reshape(count_rows, client_count, length // client_count, breadth)
-    arrived = jnp.take(over_clients(pieces), group_order, axis=1)
-    return over_groups(arrived).reshape(count_rows, length, breadth)
-
-
-def relay_back(stacked, inverse, client_count):
-    count_rows, length, breadth = stacked.shape
-    pieces = stacked.reshape(count_rows, client_count, length // client_count, breadth)
-    arrived = jnp.take(over_groups(pieces), inverse, axis=1)
-    return over_clients(arrived).reshape(count_rows, length, breadth)
-
-
-def share_sum(partial_rows):
-    return lax.psum_scatter(
-        partial_rows.astype(jnp.bfloat16), "tensor", scatter_dimension=1, tiled=True
-    ).astype(jnp.float32)
-
-
-def widen_rows(stacked):
-    return lax.all_gather(stacked, "tensor", axis=2, tiled=True)
+def greet(others):
+    barrier = pltpu.get_barrier_semaphore()
+    for other in others:
+        pl.semaphore_signal(barrier, inc=1, device_id=other, device_id_type=MESH)
+    pl.semaphore_wait(barrier, len(others))
+
+
+def send(source, target, send_sem, recv_sem, device):
+    copy = pltpu.make_async_remote_copy(
+        src_ref=source,
+        dst_ref=target,
+        send_sem=send_sem,
+        recv_sem=recv_sem,
+        device_id=device,
+        device_id_type=MESH,
+    )
+    copy.start()
+    return copy
+
+
+def place():
+    tensor_at = lax.axis_index("tensor")
+    return tensor_at // CORES, lax.rem(tensor_at, CORES)
+
+
+def turned(index, step, count):
+    return lax.rem(index + step, count)
+
+
+def columns_of(chip, core, width):
+    return pl.ds(pl.multiple_of((chip * CORES + core) * width, width), width)
+
+
+def partners(chips, client_count, group_count):
+    chip, core = place()
+    client, group = lax.axis_index("client"), lax.axis_index("sdata")
+    others = [{"tensor": chip * CORES + 1 - core}]
+    others += [{"tensor": turned(chip, k, chips) * CORES + core} for k in range(1, chips)]
+    others += [{"client": turned(client, k, client_count)} for k in range(1, client_count)]
+    others += [{"sdata": turned(group, k, group_count)} for k in range(1, group_count)]
+    return others
+
+
+class ShareSum:
+    def __init__(self, part, pair, relay, landed, sems, chunks, chips):
+        self.part, self.pair, self.relay, self.landed = part, pair, relay, landed
+        self.pair_send, self.pair_recv, self.chip_send, self.chip_recv = sems
+        self.chips, self.width = chips, part.shape[-1] // (CORES * chips)
+        self.chip, self.core = place()
+        self.copies = []
+        self.pair_copies = {}
+        self.chip_copies = {}
+        for n, q in enumerate(chunks):
+            for k in list(range(1, chips)) + [0]:
+                to = turned(self.chip, k, chips)
+                copy = send(
+                    part.at[q, :, columns_of(to, 1 - self.core, self.width)],
+                    pair.at[k, q],
+                    self.pair_send.at[k, n],
+                    self.pair_recv.at[k, n],
+                    {"tensor": self.chip * CORES + 1 - self.core},
+                )
+                self.pair_copies[k, n] = copy
+        for n, q in enumerate(chunks):
+            for k in range(1, chips):
+                to = turned(self.chip, k, chips)
+                self.pair_copies[k, n].wait_recv()
+                relay[k, q] = (
+                    part[q, :, columns_of(to, self.core, self.width)].astype(F32)
+                    + pair[k, q].astype(F32)
+                ).astype(BF16)
+                self.chip_copies[k, n] = send(
+                    relay.at[k, q],
+                    landed.at[k, q],
+                    self.chip_send.at[k, n],
+                    self.chip_recv.at[k, n],
+                    {"tensor": to * CORES + self.core},
+                )
+
+    def get(self, n, q):
+        self.pair_copies[0, n].wait_recv()
+        total = self.part[q, :, columns_of(self.chip, self.core, self.width)].astype(
+            F32
+        ) + self.pair[0, q].astype(F32)
+        for k in range(1, self.chips):
+            self.chip_copies[k, n].wait_recv()
+            total = total + self.landed[k, q].astype(F32)
+        return total
+
+    def finish(self):
+        for copy in list(self.pair_copies.values()) + list(self.chip_copies.values()):
+            copy.wait_send()
+
+
+class Widen:
+    def __init__(self, out, sems, chips):
+        self.out, self.chips = out, chips
+        self.chip_send, self.chip_recv, self.pair_send, self.pair_recv = sems
+        self.chip, self.core = place()
+        self.width = out.shape[-1] // (CORES * chips)
+        self.started, self.forwarded, self.chip_copies = [], [], {}
+
+    def pair_copy(self, source, k, n, q):
+        cols = columns_of(turned(self.chip, self.chips - k, self.chips), self.core, self.width)
+        self.forwarded.append(
+            send(
+                source,
+                self.out.at[q, :, cols],
+                self.pair_send.at[k, n],
+                self.pair_recv.at[k, n],
+                {"tensor": self.chip * CORES + 1 - self.core},
+            )
+        )
+
+    def start(self, source, n, q):
+        cols = columns_of(self.chip, self.core, self.width)
+        for k in range(1, self.chips):
+            self.chip_copies[k, n] = send(
+                source,
+                self.out.at[q, :, cols],
+                self.chip_send.at[k, n],
+                self.chip_recv.at[k, n],
+                {"tensor": turned(self.chip, k, self.chips) * CORES + self.core},
+            )
+        self.pair_copy(source, 0, n, q)
+        self.out[q, :, cols] = source[...]
+
+    def forward(self, n, q):
+        for k in range(1, self.chips):
+            self.chip_copies[k, n].wait_recv()
+            cols = columns_of(turned(self.chip, self.chips - k, self.chips), self.core, self.width)
+            self.pair_copy(self.out.at[q, :, cols], k, n, q)
+
+    def finish(self):
+        for copy in self.forwarded:
+            copy.wait_recv()
+        for copy in self.forwarded + list(self.chip_copies.values()):
+            copy.wait_send()
+
+
+def out_kernel(
+    chips, client_count, group_count,
+    order, part, inputs, upstream,
+    cut_out, up_out, up_own,
+    pair, relay, landed, cut_from, cut_at, up_at, cut_put, up_put, cut_own,
+    tp_sems, z_sems, y_sems, wide_sems,
+):
+    client, group = lax.axis_index("client"), lax.axis_index("sdata")
+    chip, core = place()
+    share = client_count // group_count
+    width = part.shape[-1] // (CORES * chips)
+    cols = columns_of(chip, core, width)
+    greet(partners(chips, client_count, group_count))
+    steps = list(range(1, client_count)) + [0]
+    targets = [turned(client, k, client_count) for k in steps]
+    up_z = []
+    sums = ShareSum(part, pair, relay, landed, [tp_sems.at[i] for i in range(4)], targets, chips)
+    for k in range(1, client_count):
+        to = turned(client, k, client_count)
+        up_z.append(
+            send(
+                upstream.at[to, :, cols], up_at.at[client],
+                z_sems.at[0, k], z_sems.at[1, k], {"client": to},
+            )
+        )
+    up_at[client] = upstream[client, :, cols]
+    cut_z = []
+    for n, (k, to) in enumerate(zip(steps, targets)):
+        block = (sums.get(n, to) + inputs[to, :, cols].astype(F32)).astype(BF16)
+        if k == 0:
+            cut_at[client] = block
+        else:
+            cut_from[k] = block
+            cut_z.append(
+                send(
+                    cut_from.at[k], cut_at.at[client],
+                    z_sems.at[2, k], z_sems.at[3, k], {"client": to},
+                )
+            )
+    widens = [
+        Widen(up_out, [wide_sems.at[i] for i in range(4)], chips),
+        Widen(cut_out, [wide_sems.at[i] for i in range(4, 8)], chips),
+    ]
+    rounds = []
+    for which, (z_copies, at, put, own) in enumerate(
+        ((up_z, up_at, up_put, up_own), (cut_z, cut_at, cut_put, cut_own))
+    ):
+        for copy in z_copies:
+            copy.wait_recv()
+        y_copies = []
+        for d in range(1, group_count):
+            to = turned(group, d, group_count)
+            for i in range(share):
+                put[d, i] = at[order[to * share + i]]
+                y_copies.append(
+                    (
+                        send(
+                            put.at[d, i], own.at[group * share + i],
+                            y_sems.at[2 * which, d, i], y_sems.at[2 * which + 1, d, i],
+                            {"sdata": to},
+                        ),
+                        turned(group, group_count - d, group_count) * share + i,
+                    )
+                )
+        n = 0
+        for i in range(share):
+            q = group * share + i
+            own[q] = at[order[group * share + i]]
+            widens[which].start(own.at[q], n, q)
+            rounds.append((which, n, q))
+            n += 1
+        for copy, q in y_copies:
+            copy.wait_recv()
+            widens[which].start(own.at[q], n, q)
+            rounds.append((which, n, q))
+            n += 1
+        for copy, q in y_copies:
+            copy.wait_send()
+    for which, n, q in rounds:
+        widens[which].forward(n, q)
+    for widen in widens:
+        widen.finish()
+    sums.finish()
+    for copy in up_z + cut_z:
+        copy.wait_send()
+
+
+def back_kernel(
+    chips, client_count, group_count,
+    inverse, part, up_own,
+    grad_out,
+    pair, relay, landed, y_from, y_at, z_from, own,
+    tp_sems, y_sems, z_sems, wide_sems,
+):
+    client, group = lax.axis_index("client"), lax.axis_index("sdata")
+    share = client_count // group_count
+    greet(partners(chips, client_count, group_count))
+    steps = [(d, i) for d in list(range(1, group_count)) + [0] for i in range(share)]
+    chunks = [turned(group, d, group_count) * share + i for d, i in steps]
+    sums = ShareSum(part, pair, relay, landed, [tp_sems.at[i] for i in range(4)], chunks, chips)
+    y_copies = []
+    for n, ((d, i), q) in enumerate(zip(steps, chunks)):
+        block = (sums.get(n, q) + up_own[q].astype(F32)).astype(BF16)
+        if d == 0:
+            y_at[group * share + i] = block
+        else:
+            y_from[d, i] = block
+            y_copies.append(
+                send(
+                    y_from.at[d, i], y_at.at[group * share + i],
+                    y_sems.at[0, d, i], y_sems.at[1, d, i],
+                    {"sdata": turned(group, d, group_count)},
+                )
+            )
+    for copy in y_copies:
+        copy.wait_recv()
+    widen = Widen(grad_out, [wide_sems.at[i] for i in range(4)], chips)
+    z_copies = []
+    for k in list(range(1, client_count)):
+        to = turned(client, k, client_count)
+        z_from[k] = y_at[inverse[to]]
+        z_copies.append(
+            send(
+                z_from.at[k], own.at[client], z_sems.at[0, k], z_sems.at[1, k], {"client": to}
+            )
+        )
+    own[client] = y_at[inverse[client]]
+    widen.start(own.at[client], 0, client)
+    for k, copy in enumerate(z_copies, 1):
+        copy.wait_recv()
+        source = turned(client, client_count - k, client_count)
+        widen.start(own.at[source], k, source)
+    for k in range(client_count):
+        widen.forward(k, turned(client, client_count - k, client_count))
+    widen.finish()
+    sums.finish()
+    for copy in y_copies + z_copies:
+        copy.wait_send()
+
+
+def average_kernel(client_count, group_count, count, *refs):
+    grads, outs = refs[:count], refs[count : 2 * count]
+    y_at, z_from, z_at = (refs[(2 + i) * count : (3 + i) * count] for i in range(3))
+    y_sems, z_sems = refs[5 * count :]
+    client, group = lax.axis_index("client"), lax.axis_index("sdata")
+    others = [{"client": turned(client, k, client_count)} for k in range(1, client_count)]
+    others += [{"sdata": turned(group, k, group_count)} for k in range(1, group_count)]
+    greet(others)
+    middle = client_count // 2
+    steps = [(middle + k) % client_count for k in range(client_count)]
+    steps = [k for k in steps if k != 0] + [0]
+    y_copies = {}
+    for k in steps:
+        to = turned(client, k, client_count)
+        for a in range(count):
+            for d in range(1, group_count):
+                y_copies[k, a, d] = send(
+                    grads[a].at[to, turned(group, d, group_count)], y_at[a].at[d, to],
+                    y_sems.at[0, a, d, k], y_sems.at[1, a, d, k],
+                    {"sdata": turned(group, d, group_count)},
+                )
+    z_copies = []
+    rows = outs[0].shape[0]
+    block = next(b for b in (64, 32, 16, rows) if rows % b == 0)
+    for k in steps:
+        to = turned(client, k, client_count)
+        for a in range(count):
+            for d in range(1, group_count):
+                y_copies[k, a, d].wait_recv()
+            for r in range(0, rows, block):
+                at = pl.ds(r, block)
+                total = grads[a][to, group, at, :].astype(F32)
+                for d in range(1, group_count):
+                    total = total + y_at[a][d, to, at, :].astype(F32)
+                z_from[a][k, at, :] = total.astype(BF16)
+            if k != 0:
+                z_copies.append(
+                    send(
+                        z_from[a].at[k], z_at[a].at[k],
+                        z_sems.at[0, a, k], z_sems.at[1, a, k], {"client": to},
+                    )
+                )
+    for copy in z_copies:
+        copy.wait_recv()
+    for a in range(count):
+        for r in range(0, rows, block):
+            at = pl.ds(r, block)
+            total = z_from[a][0, at, :].astype(F32)
+            for k in range(1, client_count):
+                total = total + z_at[a][k, at, :].astype(F32)
+            outs[a][at, :] = (total * (1.0 / client_count)).astype(BF16)
+    for copy in list(y_copies.values()) + z_copies:
+        copy.wait_send()
+
+
+VMEM_SPEC = pl.BlockSpec(memory_space=pltpu.VMEM)
+SMEM_SPEC = pl.BlockSpec(memory_space=pltpu.SMEM)
+
+
+def params(number):
+    return pltpu.CompilerParams(
+        collective_id=number, has_side_effects=True, vmem_limit_bytes=48 * 2**20
+    )
+
+
+def axis_counts():
+    return lax.axis_size("tensor") // CORES, lax.axis_size("client"), lax.axis_size("sdata")
+
+
+def relay_out(order, attended, rows_in, upstream):
+    chips, client_count, group_count = axis_counts()
+    length, breadth = rows_in.shape
+    chunk, width = length // client_count, breadth // (CORES * chips)
+    share = client_count // group_count
+    full = (client_count, chunk, breadth)
+    own = (client_count, chunk, width)
+    dma = pltpu.SemaphoreType.DMA
+    vmem = lambda shape: pltpu.VMEM(shape, BF16)
+    cut, up, up_own = pl.pallas_call(
+        partial(out_kernel, chips, client_count, group_count),
+        out_shape=(
+            jax.ShapeDtypeStruct(full, BF16),
+            jax.ShapeDtypeStruct(full, BF16),
+            jax.ShapeDtypeStruct(own, BF16),
+        ),
+        in_specs=[SMEM_SPEC, VMEM_SPEC, VMEM_SPEC, VMEM_SPEC],
+        out_specs=(VMEM_SPEC,) * 3,
+        scratch_shapes=[
+            vmem((chips,) + own), vmem((chips,) + own), vmem((chips,) + own),
+            vmem(own), vmem(own), vmem(own),
+            vmem((group_count, share, chunk, width)), vmem((group_count, share, chunk, width)),
+            vmem(own),
+            dma((4, chips, client_count)), dma((4, client_count)),
+            dma((4, group_count, share)), dma((8, chips, client_count)),
+        ],
+        compiler_params=params(1),
+        name="relay_out",
+    )(order, attended.reshape(full), rows_in.reshape(full), upstream.reshape(full))
+    return cut.reshape(length, breadth), up.reshape(length, breadth), up_own
+
+
+def relay_back(inverse, pulled, up_own):
+    chips, client_count, group_count = axis_counts()
+    length, breadth = pulled.shape
+    chunk, width = length // client_count, breadth // (CORES * chips)
+    share = client_count // group_count
+    full = (client_count, chunk, breadth)
+    own = (client_count, chunk, width)
+    dma = pltpu.SemaphoreType.DMA
+    vmem = lambda shape: pltpu.VMEM(shape, BF16)
+    grad = pl.pallas_call(
+        partial(back_kernel, chips, client_count, group_count),
+        out_shape=jax.ShapeDtypeStruct(full, BF16),
+        in_specs=[SMEM_SPEC, VMEM_SPEC, VMEM_SPEC],
+        out_specs=VMEM_SPEC,
+        scratch_shapes=[
+            vmem((chips,) + own), vmem((chips,) + own), vmem((chips,) + own),
+            vmem((group_count, share, chunk, width)), vmem(own), vmem(own), vmem(own),
+            dma((4, chips, client_count)), dma((2, group_count, share)),
+            dma((2, client_count)), dma((4, chips, client_count)),
+        ],
+        compiler_params=params(2),
+        name="relay_back",
+    )(inverse, pulled.reshape(full), up_own)
+    return grad.reshape(length, breadth)
+
+
+def average(grads):
+    unused, client_count, group_count = axis_counts()
+    count = len(grads)
+    rows = grads[0].shape[0] // (client_count * group_count)
+    widths = [grad.shape[1] for grad in grads]
+    dma = pltpu.SemaphoreType.DMA
+    return pl.pallas_call(
+        partial(average_kernel, client_count, group_count, count),
+        out_shape=tuple(jax.ShapeDtypeStruct((rows, width), BF16) for width in widths),
+        in_specs=[VMEM_SPEC] * count,
+        out_specs=(VMEM_SPEC,) * count,
+        scratch_shapes=[pltpu.VMEM((group_count, client_count, rows, w), BF16) for w in widths]
+        + [pltpu.VMEM((client_count, rows, w), BF16) for w in widths]
+        + [pltpu.VMEM((client_count, rows, w), BF16) for w in widths]
+        + [dma((2, count, group_count, client_count)), dma((2, count, client_count))],
+        compiler_params=params(3),
+        name="average",
+    )(*[grad.reshape(client_count, group_count, rows, grad.shape[1]) for grad in grads])
 
 
 def local(
@@ -155,45 +556,23 @@
         client_value_weight[0],
         output_weight[0],
     )
-    group_order = jnp.argsort(assignment, stable=True)
-    inverse = jnp.argsort(group_order, stable=True)
-    shard_width = client_input.shape[1] // lax.axis_size("tensor")
-    shard_start = lax.axis_index("tensor") * shard_width
-    own_input = lax.dynamic_slice_in_dim(client_input, shard_start, shard_width, 1)
-    own_upstream = lax.dynamic_slice_in_dim(upstream, shard_start, shard_width, 1)
-    cut_input = (own_input.astype(jnp.float32) + share_sum(attended)).astype(jnp.bfloat16)
-    arrived = relay_out(jnp.stack([cut_input, own_upstream]), group_order, client_count)
-    widened = widen_rows(arrived)
+    ids = jnp.arange(client_count).astype(jnp.int32)
+    ahead = (assignment[None, :] < assignment[:, None]) | (
+        (assignment[None, :] == assignment[:, None]) & (ids[None, :] < ids[:, None])
+    )
+    inverse = jnp.sum(ahead.astype(jnp.int32), 1)
+    group_order = jnp.sum(jnp.where(inverse[None, :] == ids[:, None], ids[None, :], 0), 1)
+    cut_rows, up_rows, up_own = relay_out(
+        group_order, attended.astype(BF16), client_input, upstream
+    )
     pulled = server_pull(
-        widened[0], widened[1], server_gain[0], server_gate[0], server_up[0], server_down[0]
-    )
-    cut_grad = (share_sum(pulled) + arrived[1].astype(jnp.float32)).astype(jnp.bfloat16)
-    returned = relay_back(cut_grad[None], inverse, client_count)
-    arriving_grad = widen_rows(returned)[0]
+        cut_rows, up_rows, server_gain[0], server_gate[0], server_up[0], server_down[0]
+    )
+    arriving_grad = relay_back(inverse, pulled.astype(BF16), up_own)
     query_grad, key_grad, value_grad, output_grad = pullback(arriving_grad.astype(jnp.float32))
-    query_width = query_grad.shape[1]
-    key_width = key_grad.shape[1]
-    joined_grads = jnp.concatenate(
-        [
-            query_grad.astype(jnp.float32),
-            key_grad.astype(jnp.float32),
-            value_grad.astype(jnp.float32),
-            output_grad.astype(jnp.float32),
-        ],
-        1,
-    )
-    summed = (
-        lax.psum_scatter(
-            joined_grads.astype(jnp.bfloat16), ("client", "sdata"), scatter_dimension=0, tiled=True
-        ).astype(jnp.float32)
-        / client_count
-    )
-    query_update = summed[:, :query_width].astype(jnp.bfloat16)
-    key_update = summed[:, query_width : query_width + key_width].astype(jnp.bfloat16)
-    value_update = summed[:, query_width + key_width : query_width + 2 * key_width].astype(
-        jnp.bfloat16
-    )
-    output_update = summed[:, query_width + 2 * key_width :].astype(jnp.bfloat16)
+    output_update, query_update, key_update, value_update = average(
+        [output_grad, query_grad, key_grad, value_grad]
+    )
     return (query_update, key_update, value_update, output_update)
 
 

time: 378 us -> 220 us (0.58)
  waiting for transfers between devices: 223 us -> 0 us
  Pallas kernels: 0 us -> 141 us
  blocking collectives: 26.1 us -> 0 us
  other arithmetic: 32.9 us -> 12 us
  between operations: 14.4 us -> 1.2 us
  starting transfers between devices: 9.16 us -> 0 us
    reduce_scatter x3 -> x0, waiting for transfers between devices: 157 us -> none  [the longest x1 104 us: local(): lax.psum_scatter(joined_grads.astype(jnp.bfloat16), ('client', 'sdata'),...]
    pallas_call x0 -> x3, Pallas kernels: none -> 141 us  [the longest x1 69.7 us: average(): pl.pallas_call(partial(average_kernel, client_count, group_count, count),...]
    all_gather x2 -> x0, waiting for transfers between devices: 45.7 us -> none  [widen_rows(): return lax.all_gather(stacked, 'tensor', axis=2, tiled=True)]
    all_to_all x2 -> x0, blocking collectives: 26.1 us -> none  [the longest x1 13.9 us: over_clients(): lax.all_to_all(pieces, 'client', split_axis=1, concat_axis=1, tiled=True)]
    all_to_all x2 -> x0, waiting for transfers between devices: 20.2 us -> none  [the longest x1 14.2 us: over_clients(): lax.all_to_all(pieces, 'client', split_axis=1, concat_axis=1, tiled=True)]
    concatenate x1 -> x0, other arithmetic: 10.1 us -> none  [local(): jnp.concatenate([query_grad.astype(jnp.float32), key_grad.astype(jnp.floa...]
    all_to_all x2 -> x0, starting transfers between devices: 8.59 us -> none  [the longest x1 5.13 us: over_clients(): lax.all_to_all(pieces, 'client', split_axis=1, concat_axis=1, tiled=True)]
    unnamed x62 -> x50, local copies, waits for them, and re-layouts: 11.7 us -> 13.8 us
  transfers between devices with their start and end apart: 7 -> 0, of which waited for: 7 -> 0; matrix products, arithmetic and copies ran while one was open for 2% -> 0% of each run, Pallas kernels for 0% -> 0%
where the time goes in v1:
time: 220 us; the launch traced here: 218 us
  Pallas kernels  141 us (64%)
  matrix products  48.9 us (22%)
  local copies, waits for them, and re-layouts  15.1 us (7%)
  other arithmetic  12 us (5%)
    pallas_call x1, Pallas kernels, average(): pl.pallas_call(partial(average_kernel, client_count, group_count, count),...  69.7 us
    pallas_call x1, Pallas kernels, relay_out(): pl.pallas_call(partial(out_kernel, chips, client_count, group_count), out...  42.2 us
    pallas_call x1, Pallas kernels, relay_back(): pl.pallas_call(partial(back_kernel, chips, client_count, group_count), ou...  28.8 us
    unnamed x50, local copies, waits for them, and re-layouts  13.8 us
    dot_general x1, matrix products, server_pull(): lax.dot_general(gate_grad, gate_matrix, (((1,), (1,)), ((), ())), preferr...  10.1 us
    dot_general x1, matrix products, server_pull(): lax.dot_general(up_grad, up_matrix, (((1,), (1,)), ((), ())), preferred_e...  8.16 us
    dot_general x3, matrix products, attention_part(): jnp.einsum('grqk,kgd->qgrd', weights.astype(jnp.float32), value_heads.ast...  7.32 us
    dot_general x2, matrix products, attention_part(): jnp.dot(normed, query_matrix, preferred_element_type=jnp.float32)  4.86 us

profile of v1, /device:TPU:8, one launch (start us, length us, event | category | flops | bytes accessed | tf_op | source)
XLA Modules:
  0.0 217.9 jit_solution(5825850895424538521)
XLA Ops:
  0.6 0.9 mul.312
  1.5 1.8 fusion.18
  3.3 4.0 %copy.27 = bf16[1,2048,512]{1,2,0:T(8,128)(2,1)} copy(bf16[1,2048,512]{2,1,0:T(8,128)(2,1)} %param.14) | data formatting | bytes 4194304 | tf_op args[2]
  7.3 3.4 %fusion.34 = f32[384,8,64]{0,2,1:T(8,128)S(1)} fusion(bf16[8,64,2048]{2,1,0:T(8,128)(2,1)} %bitcast.184, bf16[384,2048]{1,0:T(8,128)(2,1)} %param.12, f32[2048]{0:T(1024)S(1)} %bitcast.202, f32[384]{0:T(512)S(1)} %add_rsqrt_fusion.1), kind=kOutput, calls=%fused_computation.50 | convolution fusion | flops 808452096 | bytes 4466176 | tf_op jit(solution)/shard_map/jvp()/dot_general | solution.py:47
  10.8 0.3 multiply_cosine_fusion
  11.1 0.2 fusion.50
  11.2 2.0 copy.26
  13.3 2.2 %fusion.36 = f32[384,2,64]{0,2,1:T(8,128)S(1)} fusion(bf16[2,64,2048]{2,1,0:T(8,128)(2,1)} %bitcast.190, bf16[384,2048]{1,0:T(8,128)(2,1)} %param.12, f32[2048]{0:T(1024)S(1)} %bitcast.203, f32[384]{0:T(512)S(1)} %add_rsqrt_fusion.1), kind=kOutput, calls=%fused_computation.52 | convolution fusion | flops 204472320 | bytes 2303488 | tf_op jit(solution)/shard_map/jvp()/dot_general | solution.py:55
  15.6 0.9 fusion.7
  16.5 1.0 fusion.30
  17.5 1.1 divide_convert_fusion
  18.7 0.9 copy-done.6
  19.5 0.1 copy-done.18
  19.6 0.7 convolution_convert_fusion.8
  20.4 0.5 convolution_convert_fusion.7
  21.0 1.0 convolution_convert_fusion.2
  22.0 0.2 convert_reduce_fusion.inverse
  22.2 0.1 select_reduce_fusion.order
  22.3 42.2 %relay_out.1 = (bf16[4,96,2048]{2,1,0:T(8,128)(2,1)S(1)}, bf16[4,96,2048]{2,1,0:T(8,128)(2,1)S(1)}, bf16[4,96,512]{2,1,0:T(8,128)(2,1)S(1)}) custom-call(s32[4]{0:T(128)S(1)} %select_reduce_fusion.order, bf16[4,96,2048]{2,1,0:T(8,128)(2,1)S(1)} %bitcast.173, bf16[4,96,2048]{2,1,0:T(8,128)(2,1)} %bitcast.181, bf16[4,96,2048]{2,1,0:T(8,128)(2,1)} %bitcast.185), custom_call_target="tpu_custom_call" | custom-call | tf_op jit(solution)/shard_map/relay_out/pallas_call | solution.py:467
  64.6 0.4 fusion.21
  65.0 0.4 fusion.23
  65.5 2.4 %copy-done.17 = bf16[1,2048,1024]{2,1,0:T(8,128)(2,1)S(1)} copy-done((bf16[1,2048,1024]{2,1,0:T(8,128)(2,1)S(1)}, bf16[1,2048,1024]{2,1,0:T(8,128)(2,1)}, u32[]{:S(2)}) %copy-start.17) | copy-done | bytes 4194328
  67.9 3.0 %fusion.10 = f32[384,1024]{1,0:T(8,128)} fusion(bf16[384,2048]{1,0:T(8,128)(2,1)S(1)} %bitcast.186, bf16[1,2048,1024]{2,1,0:T(8,128)(2,1)S(1)} %copy-done.17), kind=kOutput, calls=%fused_computation.15 | convolution fusion | flops 1610612736 | bytes 7340032 | tf_op jit(solution)/shard_map/dot_general | solution.py:87
  70.9 3.1 %fusion.16 = f32[384,1024]{1,0:T(8,128)} fusion(bf16[384,2048]{1,0:T(8,128)(2,1)S(1)} %bitcast.178, bf16[1,1024,2048]{2,1,0:T(8,128)(2,1)S(1)} %copy-done.16), kind=kOutput, calls=%fused_computation.21 | convolution fusion | flops 1610612736 | bytes 7340032 | tf_op jit(solution)/shard_map/dot_general | solution.py:89
  74.1 10.1 %fusion.8 = f32[384,2048]{1,0:T(8,128)} fusion(bf16[1,2048,1024]{2,1,0:T(8,128)(2,1)} %param.19, f32[384,1024]{1,0:T(8,128)} %fusion.10, f32[384,1024]{1,0:T(8,128)} %fusion.16, bf16[384,2048]{1,0:T(8,128)(2,1)} %bitcast.187, bf16[1,2048,1024]{2,1,0:T(8,128)(2,1)} %param.20), kind=kOutput, calls=%fused_computation.13 | convolution fusion | flops 3225157632 | bytes 16252928 | tf_op jit(solution)/shard_map/dot_general | solution.py:97
  84.2 8.2 %fusion.27 = (f32[384]{0:T(512)S(1)}, f32[384,2048]{1,0:T(8,128)}) fusion(bf16[4,96,2048]{2,1,0:T(8,128)(2,1)} %copy-done.1, f32[2048]{0:T(1024)S(1)} %bitcast.201, f32[384,2048]{1,0:T(8,128)} %fusion.8, bf16[1,2048,1024]{2,1,0:T(8,128)(2,1)} %param.20, f32[384,1024]{1,0:T(8,128)} %fusion.16, f32[384,1024]{1,0:T(8,128)} %fusion.10), kind=kOutput, calls=%fused_computation.38 | convolution fusion | flops 1616903808 | bytes 15214080 | tf_op jit(solution)/shard_map/dot_general | solution.py:100
  92.4 0.1 rsqrt.25
  92.4 3.0 %fusion.26 = bf16[384,2048]{1,0:T(8,128)(2,1)S(1)} fusion(bf16[4,96,2048]{2,1,0:T(8,128)(2,1)} %copy-done.1, f32[384,2048]{1,0:T(8,128)} %get-tuple-element.31, f32[384]{0:T(512)S(1)} %broadcast_multiply_fusion, f32[384]{0:T(512)S(1)} %multiply_multiply_fusion, f32[384]{0:T(512)S(1)} %rsqrt.25), kind=kLoop, calls=%fused_computation.37 | loop fusion | flops 4718592 | bytes 6296064 | tf_op jit(solution)/shard_map/convert_element_type | solution.py:571
  95.4 28.8 %relay_back.1 = bf16[4,96,2048]{2,1,0:T(8,128)(2,1)S(1)} custom-call(s32[4]{0:T(128)S(1)} %convert_reduce_fusion.inverse, bf16[4,96,2048]{2,1,0:T(8,128)(2,1)S(1)} %bitcast.170, bf16[4,96,512]{2,1,0:T(8,128)(2,1)S(1)} %get-tuple-element.13.up_own), custom_call_target="tpu_custom_call" | custom-call | tf_op jit(solution)/shard_map/relay_back/pallas_call | solution.py:499
  124.2 1.2 copy-done.2
  125.4 1.7 fusion.40
  127.1 1.2 copy.29
  128.4 2.7 %fusion.46 = bf16[2,64,384]{2,1,0:T(8,128)(2,1)S(1)} fusion(bf16[2,64,4,384]{3,1,2,0:T(8,128)(2,1)S(1)} %bitcast.188, bf16[2,4,384,384]{2,3,1,0:T(8,128)(2,1)} %copy-done.5), kind=kOutput, calls=%fused_computation.65 | convolution fusion | flops 151044096 | bytes 2850816 | tf_op jit(solution)/shard_map/transpose(jvp(grqk,kgd->qgrd))/dot_general | solution.py:73
  131.0 2.2 %convolution_convert_fusion.3 = bf16[2048,128]{1,0:T(8,128)(2,1)S(1)} fusion(bf16[384,128]{0,1:T(8,128)(2,1)S(1)} %bitcast.198, bf16[384,2048]{1,0:T(8,128)(2,1)} %param.12, f32[2048]{0:T(1024)S(1)} %bitcast.205, f32[384]{0:T(512)S(1)} %add_rsqrt_fusion.1), kind=kOutput, calls=%fused_computation.44 | convolution fusion | flops 204734464 | bytes 2205184 | tf_op jit(solution)/shard_map/transpose(jvp())/dot_general | solution.py:60
  133.3 4.1 %fusion.6 = (f32[2,4,384]{2,1,0:T(4,128)S(1)}, bf16[2,4,384,384]{2,3,1,0:T(8,128)(2,1)S(1)}) fusion(f32[2,384,384,4]{2,1,3,0:T(8,128)} %copy-done.4, f32[2,4,384]{2,1,0:T(4,128)S(1)} %multiply_divide_fusion, f32[2,4,384]{2,1,0:T(4,128)S(1)} %get-tuple-element.28, pred[384,384]{0,1:T(8,128)(4,1)S(1)} %iota_compare_fusion.1, ...), kind=kOutput, calls=%fused_computation.8 | convolution fusion | flops 160429056 | bytes 7753728 | tf_op jit(solution)/shard_map/transpose(jvp(grqk,kgd->qgrd))/dot_general | solution.py:73
  137.5 2.2 fusion.4
  139.7 0.8 fusion.45
  140.6 0.5 copy-done.7
  141.1 0.8 convolution_convert_fusion.4
  141.9 0.5 fusion.43
  142.6 0.1 fusion.52
  142.7 1.4 convolution_convert_fusion
  144.2 1.3 convolution_convert_fusion.1
  145.5 69.7 %average.1 = (bf16[256,512]{1,0:T(8,128)(2,1)S(1)}, bf16[256,512]{1,0:T(8,128)(2,1)S(1)}, bf16[256,128]{1,0:T(8,128)(2,1)S(1)}, bf16[256,128]{1,0:T(8,128)(2,1)S(1)}) custom-call(bf16[4,2,256,512]{3,2,1,0:T(8,128)(2,1)S(1)} %bitcast.172, bf16[4,2,256,512]{3,2,1,0:T(8,128)(2,1)S(1)} %bitcast.171, bf16[4,2,256,128]{3,2,1,0:T(8,128)(2,1)S(1)} %bitcast.177, ...), custom_call_target="tpu_custom_call" | custom-call | tf_op jit(solution)/shard_map/average/pallas_call | solution.py:522
  215.3 0.7 copy.41
  216.0 0.6 copy.42
  216.6 0.6 copy.43
  217.2 0.7 copy.44
  (60 shorter events, 0.6 us)
Async XLA Ops:
  0.6 20.3 %copy-start = (bf16[1,2048,512]{2,1,0:T(8,128)(2,1)S(1)}, bf16[1,2048,512]{2,1,0:T(8,128)(2,1)}, u32[]{:S(2)}) copy-start(bf16[1,2048,512]{2,1,0:T(8,128)(2,1)} %param.17) | copy-start | bytes 6291460
  16.5 2.2 copy-start.4
  17.5 2.0 copy-start.6
  17.5 2.1 copy-start.18
  19.6 2.4 %copy-start.5 = (bf16[2,4,384,384]{2,3,1,0:T(8,128)(2,1)}, bf16[2,4,384,384]{2,3,1,0:T(8,128)(2,1)S(1)}, u32[]{:S(2)}) copy-start(bf16[2,4,384,384]{2,3,1,0:T(8,128)(2,1)S(1)} %divide_convert_fusion) | copy-start | bytes 7077892
  20.4 1.7 copy-start.13
  20.4 1.7 copy-start.19
  20.9 1.1 copy-start.11
  22.3 42.7 %copy-start.15 = (bf16[1,2048]{1,0:T(2,128)(2,1)S(1)}, bf16[1,2048]{1,0:T(2,128)(2,1)}, u32[]{:S(2)}) copy-start(bf16[1,2048]{1,0:T(2,128)(2,1)} %param.18) | copy-start | bytes 12292
  64.6 6.4 %copy-start.1 = (bf16[4,96,2048]{2,1,0:T(8,128)(2,1)}, bf16[4,96,2048]{2,1,0:T(8,128)(2,1)S(1)}, u32[]{:S(2)}) copy-start(bf16[4,96,2048]{2,1,0:T(8,128)(2,1)S(1)} %get-tuple-element.11) | copy-start | bytes 4718596
  64.6 3.3 %copy-start.17 = (bf16[1,2048,1024]{2,1,0:T(8,128)(2,1)S(1)}, bf16[1,2048,1024]{2,1,0:T(8,128)(2,1)}, u32[]{:S(2)}) copy-start(bf16[1,2048,1024]{2,1,0:T(8,128)(2,1)} %param.19) | copy-start | bytes 12582916
  65.5 5.5 %copy-start.8 = (bf16[4,96,2048]{2,1,0:T(8,128)(2,1)}, bf16[4,96,2048]{2,1,0:T(8,128)(2,1)S(1)}, u32[]{:S(2)}) copy-start(bf16[4,96,2048]{2,1,0:T(8,128)(2,1)S(1)} %fusion.23) | copy-start | bytes 4718596
  67.9 3.0 %copy-start.16 = (bf16[1,1024,2048]{2,1,0:T(8,128)(2,1)S(1)}, bf16[1,1024,2048]{2,1,0:T(8,128)(2,1)}, u32[]{:S(2)}) copy-start(bf16[1,1024,2048]{2,1,0:T(8,128)(2,1)} %param.21) | copy-start | bytes 12582916
  124.2 1.2 copy-start.2
  128.3 2.7 %copy-start.9 = (bf16[384,512]{0,1:T(8,128)(2,1)}, bf16[384,512]{0,1:T(8,128)(2,1)S(1)}, u32[]{:S(2)}) copy-start(bf16[384,512]{0,1:T(8,128)(2,1)S(1)} %copy.29) | copy-start | bytes 1179652
  128.4 4.9 %copy-start.14 = (bf16[384,128]{0,1:T(8,128)(2,1)S(1)}, bf16[384,128]{0,1:T(8,128)(2,1)}, u32[]{:S(2)}) copy-start(bf16[384,128]{0,1:T(8,128)(2,1)} %copy-done.13) | copy-start | bytes 294916
  131.0 2.3 %copy-start.10 = (bf16[384,512]{0,1:T(8,128)(2,1)S(1)}, bf16[384,512]{0,1:T(8,128)(2,1)}, u32[]{:S(2)}) copy-start(bf16[384,512]{0,1:T(8,128)(2,1)} %copy-done.9) | copy-start | bytes 1179652
  133.3 4.3 %slice-start = ((s8[4718592]{0:T(1024)(128)(4,1)}), s8[4194304]{0:T(1024)(128)(4,1)S(1)}, s32[]{:S(2)}) async-start(s8[4718592]{0:T(1024)(128)(4,1)} %bitcast.179), calls=%async_computation | async-start | bytes 8388608
  133.3 4.2 %slice-start.1 = ((s8[4718592]{0:T(1024)(128)(4,1)}), s8[524288]{0:T(1024)(128)(4,1)S(1)}, s32[]{:S(2)}) async-start(s8[4718592]{0:T(1024)(128)(4,1)} %bitcast.179), calls=%async_computation.1 | async-start | bytes 1048576
  139.7 1.4 copy-start.7
  142.7 1.5 copy-start.3
  142.7 1.5 copy-start.12

commit v2 on v1

--- a/solution.py
+++ b/solution.py
@@ -79,31 +79,79 @@
     )
 
 
-def server_pull(rows_in, upstream_rows, gain, gate_matrix, up_matrix, down_matrix):
-    rows_float = rows_in.astype(jnp.float32)
-    inv_rms = lax.rsqrt(jnp.mean(rows_float * rows_float, -1, keepdims=True) + 1e-05)
-    gain_float = gain.astype(jnp.float32)
-    server_normed = (rows_float * inv_rms * gain_float).astype(jnp.bfloat16)
-    gate_value = jnp.dot(server_normed, gate_matrix, preferred_element_type=jnp.float32)
-    up_value = jnp.dot(server_normed, up_matrix, preferred_element_type=jnp.float32)
+def server_kernel(
+    rows_ref, upstream_ref, gain_ref, gate_ref, up_ref, down_ref, out_ref, normed_ref, total_ref
+):
+    step = pl.program_id(0)
+
+    def inverse_rms(rows_float):
+        return lax.rsqrt(jnp.mean(rows_float * rows_float, -1, keepdims=True) + 1e-05)
+
+    @pl.when(step == 0)
+    def _():
+        rows_float = rows_ref[...].astype(F32)
+        normed_ref[...] = (
+            rows_float * inverse_rms(rows_float) * gain_ref[...].astype(F32)
+        ).astype(BF16)
+
+    gate, up = gate_ref[...], up_ref[...]
+    crossed = (((1,), (1,)), ((), ()))
+    gate_value = jnp.dot(normed_ref[...], gate, preferred_element_type=F32)
+    up_value = jnp.dot(normed_ref[...], up, preferred_element_type=F32)
     pulled = lax.dot_general(
-        upstream_rows, down_matrix, (((1,), (1,)), ((), ())), preferred_element_type=jnp.float32
+        upstream_ref[...], down_ref[...], crossed, preferred_element_type=F32
     )
     sigmoid_gate = jax.nn.sigmoid(gate_value)
     gate_grad = (
         pulled * up_value * sigmoid_gate * (1.0 + gate_value * (1.0 - sigmoid_gate))
-    ).astype(jnp.bfloat16)
-    up_grad = (pulled * gate_value * sigmoid_gate).astype(jnp.bfloat16)
+    ).astype(BF16)
+    up_grad = (pulled * gate_value * sigmoid_gate).astype(BF16)
     normed_grad = lax.dot_general(
-        gate_grad, gate_matrix, (((1,), (1,)), ((), ())), preferred_element_type=jnp.float32
-    )
-    normed_grad = normed_grad + lax.dot_general(
-        up_grad, up_matrix, (((1,), (1,)), ((), ())), preferred_element_type=jnp.float32
-    )
-    weighted = normed_grad * gain_float
-    return inv_rms * weighted - rows_float * inv_rms**3 * jnp.mean(
-        weighted * rows_float, -1, keepdims=True
-    )
+        gate_grad, gate, crossed, preferred_element_type=F32
+    ) + lax.dot_general(up_grad, up, crossed, preferred_element_type=F32)
+
+    @pl.when(step == 0)
+    def _():
+        total_ref[...] = normed_grad
+
+    @pl.when(step > 0)
+    def _():
+        total_ref[...] += normed_grad
+
+    @pl.when(step == pl.num_programs(0) - 1)
+    def _():
+        rows_float = rows_ref[...].astype(F32)
+        inv_rms = inverse_rms(rows_float)
+        weighted = total_ref[...] * gain_ref[...].astype(F32)
+        out_ref[...] = (
+            inv_rms * weighted
+            - rows_float * inv_rms**3 * jnp.mean(weighted * rows_float, -1, keepdims=True)
+        ).astype(BF16)
+
+
+def server_pull(rows_in, upstream_rows, gain, gate_matrix, up_matrix, down_matrix):
+    length, breadth = rows_in.shape
+    hidden = gate_matrix.shape[1]
+    block = next(b for b in (256, 128, hidden) if hidden % b == 0)
+    whole = pl.BlockSpec((length, breadth), lambda i: (0, 0))
+    tall = pl.BlockSpec((breadth, block), lambda i: (0, i))
+    return pl.pallas_call(
+        server_kernel,
+        grid=(hidden // block,),
+        out_shape=jax.ShapeDtypeStruct((length, breadth), BF16),
+        in_specs=[
+            whole,
+            whole,
+            pl.BlockSpec((1, breadth), lambda i: (0, 0)),
+            tall,
+            tall,
+            pl.BlockSpec((block, breadth), lambda i: (i, 0)),
+        ],
+        out_specs=whole,
+        scratch_shapes=[pltpu.VMEM((length, breadth), BF16), pltpu.VMEM((length, breadth), F32)],
+        compiler_params=pltpu.CompilerParams(vmem_limit_bytes=48 * 2**20),
+        name="server_pull",
+    )(rows_in, upstream_rows, gain[None], gate_matrix, up_matrix, down_matrix)
 
 
 def greet(others):
@@ -387,7 +435,8 @@
 
 
 def average_kernel(client_count, group_count, count, *refs):
-    grads, outs = refs[:count], refs[count : 2 * count]
+    early, grads, outs = refs[0], refs[1 : count + 1], refs[count + 1 : 2 * count + 1]
+    refs = refs[1:]
     y_at, z_from, z_at = (refs[(2 + i) * count : (3 + i) * count] for i in range(3))
     y_sems, z_sems = refs[5 * count :]
     client, group = lax.axis_index("client"), lax.axis_index("sdata")
@@ -400,7 +449,7 @@
     y_copies = {}
     for k in steps:
         to = turned(client, k, client_count)
-        for a in range(count):
+        for a in range(1, count):
             for d in range(1, group_count):
                 y_copies[k, a, d] = send(
                     grads[a].at[to, turned(group, d, group_count)], y_at[a].at[d, to],
@@ -410,16 +459,16 @@
     z_copies = []
     rows = outs[0].shape[0]
     block = next(b for b in (64, 32, 16, rows) if rows % b == 0)
-    for k in steps:
-        to = turned(client, k, client_count)
-        for a in range(count):
-            for d in range(1, group_count):
+    for k, a in [(k, 0) for k in steps] + [(k, a) for k in steps for a in range(1, count)]:
+            to = turned(client, k, client_count)
+            for d in range(1, group_count if a else 1):
                 y_copies[k, a, d].wait_recv()
             for r in range(0, rows, block):
                 at = pl.ds(r, block)
                 total = grads[a][to, group, at, :].astype(F32)
                 for d in range(1, group_count):
-                    total = total + y_at[a][d, to, at, :].astype(F32)
+                    other = y_at[a][d, to, at, :] if a else early[d - 1, to, at, :]
+                    total = total + other.astype(F32)
                 z_from[a][k, at, :] = total.astype(BF16)
             if k != 0:
                 z_copies.append(
@@ -513,7 +562,19 @@
     return grad.reshape(length, breadth)
 
 
-def average(grads):
+def send_early(grad):
+    unused, client_count, group_count = axis_counts()
+    group = lax.axis_index("sdata")
+    blocks = grad.reshape(client_count, group_count, -1, grad.shape[1])
+    arrived = []
+    for d in range(1, group_count):
+        block = lax.dynamic_index_in_dim(blocks, turned(group, d, group_count), 1, False)
+        ring = [(g, (g + d) % group_count) for g in range(group_count)]
+        arrived.append(lax.ppermute(block, "sdata", ring))
+    return jnp.stack(arrived)
+
+
+def average(early, grads):
     unused, client_count, group_count = axis_counts()
     count = len(grads)
     rows = grads[0].shape[0] // (client_count * group_count)
@@ -522,15 +583,18 @@
     return pl.pallas_call(
         partial(average_kernel, client_count, group_count, count),
         out_shape=tuple(jax.ShapeDtypeStruct((rows, width), BF16) for width in widths),
-        in_specs=[VMEM_SPEC] * count,
+        in_specs=[VMEM_SPEC] * (count + 1),
         out_specs=(VMEM_SPEC,) * count,
-        scratch_shapes=[pltpu.VMEM((group_count, client_count, rows, w), BF16) for w in widths]
+        scratch_shapes=[
+            pltpu.VMEM((group_count, client_count, rows, w) if n else (16, 128), BF16)
+            for n, w in enumerate(widths)
+        ]
         + [pltpu.VMEM((client_count, rows, w), BF16) for w in widths]
         + [pltpu.VMEM((client_count, rows, w), BF16) for w in widths]
         + [dma((2, count, group_count, client_count)), dma((2, count, client_count))],
         compiler_params=params(3),
         name="average",
-    )(*[grad.reshape(client_count, group_count, rows, grad.shape[1]) for grad in grads])
+    )(early, *[grad.reshape(client_count, group_count, rows, grad.shape[1]) for grad in grads])
 
 
 def local(
@@ -568,10 +632,10 @@
     pulled = server_pull(
         cut_rows, up_rows, server_gain[0], server_gate[0], server_up[0], server_down[0]
     )
-    arriving_grad = relay_back(inverse, pulled.astype(BF16), up_own)
+    arriving_grad = relay_back(inverse, pulled, up_own)
     query_grad, key_grad, value_grad, output_grad = pullback(arriving_grad.astype(jnp.float32))
     output_update, query_update, key_update, value_update = average(
-        [output_grad, query_grad, key_grad, value_grad]
+        send_early(output_grad), [output_grad, query_grad, key_grad, value_grad]
     )
     return (query_update, key_update, value_update, output_update)
 

time: 220 us -> 212 us (0.964)
  matrix products: 48.9 us -> 28 us
  Pallas kernels: 141 us -> 155 us
  other arithmetic: 12 us -> 9.55 us
  waiting for transfers between devices: 0 us -> 2.25 us
    dot_general x4 -> x0, matrix products: 24.4 us -> none  [the longest x1 10.1 us: server_pull(): lax.dot_general(gate_grad, gate_matrix, (((1,), (1,)), ((), ())), preferr...]
    pallas_call x0 -> x1, Pallas kernels: none -> 20.6 us  [server_pull(): pl.pallas_call(server_kernel, grid=(hidden // block,), out_shape=jax.Shap...]
    pallas_call x1, Pallas kernels: 69.7 us -> 63.6 us  [average(): pl.pallas_call(partial(average_kernel, client_count, group_count, count),...]
    unnamed x50 -> x38, local copies, waits for them, and re-layouts: 13.8 us -> 10.2 us
    convert_element_type x2 -> x0, other arithmetic: 3.42 us -> none  [the longest x1 3 us: local(): arriving_grad = relay_back(inverse, pulled.astype(BF16), up_own)]
    dot_general x3, matrix products: 4.09 us -> 6.86 us  [attention_part(): lax.dot_general(context, output_matrix, (((1,), (1,)), ((), ())), preferr...]
    squeeze x0 -> x1, local copies, waits for them, and re-layouts: none -> 2.27 us  [send_early(): lax.dynamic_index_in_dim(blocks, turned(group, d, group_count), 1, False)]
    ppermute x0 -> x1, waiting for transfers between devices: none -> 2.25 us  [send_early(): arrived.append(lax.ppermute(block, 'sdata', ring))]
  transfers between devices with their start and end apart: 0 -> 1, of which waited for: 0 -> 1; matrix products, arithmetic and copies ran while one was open for 0% -> 10% of each run, Pallas kernels for 0% -> 0%
where the time goes in v2:
time: 212 us
  Pallas kernels  155 us (73%)
  matrix products  28 us (13%)
  local copies, waits for them, and re-layouts  14.4 us (7%)
  other arithmetic  9.55 us (5%)
  waiting for transfers between devices  2.25 us (1%)
    pallas_call x1, Pallas kernels, average(): pl.pallas_call(partial(average_kernel, client_count, group_count, count),...  63.6 us
    pallas_call x1, Pallas kernels, relay_out(): pl.pallas_call(partial(out_kernel, chips, client_count, group_count), out...  42.2 us
    pallas_call x1, Pallas kernels, relay_back(): pl.pallas_call(partial(back_kernel, chips, client_count, group_count), ou...  28.8 us
    pallas_call x1, Pallas kernels, server_pull(): pl.pallas_call(server_kernel, grid=(hidden // block,), out_shape=jax.Shap...  20.6 us
    unnamed x38, local copies, waits for them, and re-layouts  10.2 us
    dot_general x3, matrix products, attention_part(): jnp.einsum('grqk,kgd->qgrd', weights.astype(jnp.float32), value_heads.ast...  7.52 us
    dot_general x3, matrix products, attention_part(): lax.dot_general(context, output_matrix, (((1,), (1,)), ((), ())), preferr...  6.86 us
    dot_general x2, matrix products, attention_part(): jnp.dot(normed, query_matrix, preferred_element_type=jnp.float32)  6.19 us
  transfers between devices with their start and end apart: 1, of which 1 were waited for; matrix products, arithmetic and copies ran while one was open for 10% of the time, Pallas kernels for 0%

profile of v2, /device:TPU:8, one launch (start us, length us, event | category | flops | bytes accessed | tf_op | source)
XLA Modules:
  0.0 211.7 jit_solution(6918875920300330697)
XLA Ops:
  0.6 0.0 copy-start
  0.7 1.0 convert_reduce_fusion.inverse
  1.7 0.1 select_reduce_fusion.order
  1.8 1.8 fusion.8
  3.6 0.7 mul.209
  4.4 1.2 copy.26
  5.6 0.0 copy-start.6
  5.6 3.0 %convolution_convert_fusion.8 = bf16[384,128]{0,1:T(8,128)(2,1)} fusion(bf16[1,2048,128]{2,1,0:T(8,128)(2,1)} %param.16, bf16[384,2048]{1,0:T(8,128)(2,1)} %param.12, f32[2048]{0:T(1024)S(1)} %bitcast.174, f32[384]{0:T(512)S(1)} %add_rsqrt_fusion), kind=kOutput, calls=%fused_computation.41 | convolution fusion | flops 204521472 | bytes 2205184 | tf_op jit(solution)/shard_map/jvp()/dot_general | solution.py:60
  8.6 0.7 fusion.17
  9.4 4.0 %copy.27 = bf16[1,2048,512]{1,2,0:T(8,128)(2,1)} copy(bf16[1,2048,512]{2,1,0:T(8,128)(2,1)} %param.14) | data formatting | bytes 4194304 | tf_op args[2]
  13.3 3.4 %fusion.15 = f32[384,8,64]{0,2,1:T(8,128)S(1)} fusion(bf16[8,64,2048]{2,1,0:T(8,128)(2,1)} %bitcast.160, bf16[384,2048]{1,0:T(8,128)(2,1)} %param.12, f32[2048]{0:T(1024)S(1)} %bitcast.176, f32[384]{0:T(512)S(1)} %add_rsqrt_fusion), kind=kOutput, calls=%fused_computation.28 | convolution fusion | flops 808452096 | bytes 4466176 | tf_op jit(solution)/shard_map/jvp()/dot_general | solution.py:47
  16.8 0.1 slice_negate_fusion.1
  16.8 0.3 multiply_cosine_fusion
  17.2 0.2 fusion.27
  17.3 0.9 fusion.7
  18.2 1.0 fusion.11
  19.3 0.0 copy-start.13
  19.3 1.1 divide_convert_fusion
  20.4 0.5 convolution_convert_fusion.7
  21.0 1.0 convolution_convert_fusion.2
  22.1 42.2 %relay_out.1 = (bf16[4,96,2048]{2,1,0:T(8,128)(2,1)S(1)}, bf16[4,96,2048]{2,1,0:T(8,128)(2,1)S(1)}, bf16[4,96,512]{2,1,0:T(8,128)(2,1)S(1)}) custom-call(s32[4]{0:T(128)S(1)} %select_reduce_fusion.order, bf16[4,96,2048]{2,1,0:T(8,128)(2,1)S(1)} %bitcast.143, bf16[4,96,2048]{2,1,0:T(8,128)(2,1)} %bitcast.153, bf16[4,96,2048]{2,1,0:T(8,128)(2,1)} %bitcast.161), custom_call_target="tpu_custom_call" | custom-call | tf_op jit(solution)/shard_map/relay_out/pallas_call | solution.py:516
  64.3 20.6 %server_pull.1 = bf16[384,2048]{1,0:T(8,128)(2,1)S(1)} custom-call(bf16[384,2048]{1,0:T(8,128)(2,1)S(1)} %bitcast.146, bf16[384,2048]{1,0:T(8,128)(2,1)S(1)} %bitcast.147, bf16[1,2048]{1,0:T(2,128)(2,1)S(1)} %copy-done.3, bf16[2048,1024]{1,0:T(8,128)(2,1)} %bitcast.154, bf16[2048,1024]{1,0:T(8,128)(2,1)} %bitcast.155, bf16[1024,2048]{1,0:T(8,128)(2,1)} %bitcast.156), custom_call_target="tpu_custom_call" | custom-call | tf_op jit(solution)/shard_map/server_pull/pallas_call | solution.py:138
  84.9 28.8 %relay_back.1 = bf16[4,96,2048]{2,1,0:T(8,128)(2,1)S(1)} custom-call(s32[4]{0:T(128)S(1)} %convert_reduce_fusion.inverse, bf16[4,96,2048]{2,1,0:T(8,128)(2,1)S(1)} %bitcast.140, bf16[4,96,512]{2,1,0:T(8,128)(2,1)S(1)} %get-tuple-element.13.up_own), custom_call_target="tpu_custom_call" | custom-call | tf_op jit(solution)/shard_map/relay_back/pallas_call | solution.py:548
  113.7 1.1 copy-done.2
  114.8 2.7 %convolution_convert_fusion.1 = bf16[2048,512]{1,0:T(8,128)(2,1)} fusion(bf16[384,2048]{1,0:T(8,128)(2,1)S(1)} %bitcast.144, bf16[384,512]{0,1:T(8,128)(2,1)S(1)} %bitcast.166), kind=kOutput, calls=%fused_computation.19 | convolution fusion | flops 806354944 | bytes 4063232 | tf_op jit(solution)/shard_map/transpose(jvp())/dot_general | solution.py:77
  117.5 2.3 %dynamic-slice_bitcast_fusion = bf16[4,256,512]{2,1,0:T(8,128)(2,1)} fusion(bf16[4,2,256,512]{3,2,1,0:T(8,128)(2,1)} %bitcast.141, s32[]{:T(128)S(6)} %select_n.22), kind=kLoop, calls=%fused_computation.42 | loop fusion | bytes 2097156 | tf_op jit(solution)/shard_map/jit(dynamic_index_in_dim)/squeeze | solution.py:571
  119.8 1.3 collective-permute-start
  121.0 0.7 iota_compare_fusion
  121.7 3.1 %fusion.19 = bf16[384,512]{1,0:T(8,128)(2,1)} fusion(bf16[384,2048]{1,0:T(8,128)(2,1)} %bitcast.145, bf16[1,2048,512]{2,1,0:T(8,128)(2,1)S(1)} %copy-done), kind=kOutput, calls=%fused_computation.32 | convolution fusion | flops 805502976 | bytes 4063232 | tf_op jit(solution)/shard_map/transpose(jvp())/dot_general | solution.py:77
  124.9 1.9 copy.29
  126.8 2.8 %fusion.25 = bf16[2,64,384]{2,1,0:T(8,128)(2,1)S(1)} fusion(bf16[2,64,4,384]{3,1,2,0:T(8,128)(2,1)} %bitcast.162, bf16[2,4,384,384]{2,3,1,0:T(8,128)(2,1)} %copy-done.5), kind=kOutput, calls=%fused_computation.40 | convolution fusion | flops 151044096 | bytes 2850816 | tf_op jit(solution)/shard_map/transpose(jvp(grqk,kgd->qgrd))/dot_general | solution.py:73
  129.6 4.2 %fusion.6 = (f32[2,4,384]{2,1,0:T(4,128)S(1)}, bf16[2,4,384,384]{2,3,1,0:T(8,128)(2,1)S(1)}) fusion(f32[2,384,384,4]{2,1,3,0:T(8,128)} %copy-done.4, f32[2,4,384]{2,1,0:T(4,128)S(1)} %multiply_divide_fusion, f32[2,4,384]{2,1,0:T(4,128)S(1)} %get-tuple-element.28, pred[384,384]{0,1:T(8,128)(4,1)S(1)} %iota_compare_fusion.1, ...), kind=kOutput, calls=%fused_computation.8 | convolution fusion | flops 160429056 | bytes 7753728 | tf_op jit(solution)/shard_map/transpose(jvp(grqk,kgd->qgrd))/dot_general | solution.py:73
  133.9 2.2 %fusion.4 = bf16[2,384,384,4]{2,1,3,0:T(8,128)(2,1)S(1)} fusion(bf16[2,4,384,384]{2,3,1,0:T(8,128)(2,1)S(1)} %get-tuple-element.31, f32[2,384,384,4]{2,1,3,0:T(8,128)S(1)} %bitcast.152, f32[2,384,4]{1,2,0:T(4,128)S(1)} %bitcast.168, f32[2,384,4]{1,2,0:T(4,128)S(1)} %negate_bitcast_fusion, f32[2,384,4]{1,2,0:T(4,128)S(1)} %bitcast.169, ...), kind=kLoop, calls=%fused_computation.6 | loop fusion | flops 11796480 | bytes 9621504 | tf_op jit(solution)/shard_map/transpose(jvp())/mul | solution.py:64
  136.0 0.8 fusion.24
  136.9 0.5 fusion.22
  137.5 0.1 bitcast_multiply_fusion
  137.6 0.1 fusion.43
  137.6 0.1 fusion.29
  137.8 1.1 copy-done.7
  138.9 0.8 convolution_convert_fusion.3
  139.6 0.8 convolution_convert_fusion.4
  140.4 2.8 %convolution_convert_fusion = bf16[2048,512]{1,0:T(8,128)(2,1)} fusion(bf16[384,512]{0,1:T(8,128)(2,1)S(1)} %bitcast.167, bf16[384,2048]{1,0:T(8,128)(2,1)S(1)} %copy-done.7, f32[2048]{0:T(1024)S(1)} %bitcast.179, f32[384]{0:T(512)S(1)} %add_rsqrt_fusion), kind=kOutput, calls=%fused_computation.18 | convolution fusion | flops 808452096 | bytes 4072960 | tf_op jit(solution)/shard_map/transpose(jvp())/dot_general | solution.py:47
  143.2 2.2 %collective-permute-done = bf16[4,256,512]{2,1,0:T(8,128)(2,1)S(1)} collective-permute-done((bf16[4,256,512]{2,1,0:T(8,128)(2,1)}, bf16[4,256,512]{2,1,0:T(8,128)(2,1)S(1)}, u32[]{:S(2)}, u32[]{:S(2)}) %collective-permute-start) | collective-permute-done | bytes 1048608 | tf_op jit(solution)/shard_map/ppermute | solution.py:573
  145.4 63.6 %average.1 = (bf16[256,512]{1,0:T(8,128)(2,1)S(1)}, bf16[256,512]{1,0:T(8,128)(2,1)S(1)}, bf16[256,128]{1,0:T(8,128)(2,1)S(1)}, bf16[256,128]{1,0:T(8,128)(2,1)S(1)}) custom-call(bf16[1,4,256,512]{3,2,1,0:T(8,128)(2,1)S(1)} %bitcast.148, bf16[4,2,256,512]{3,2,1,0:T(8,128)(2,1)S(1)} %bitcast.142, bf16[4,2,256,512]{3,2,1,0:T(8,128)(2,1)} %bitcast.159, ...), custom_call_target="tpu_custom_call" | custom-call | tf_op jit(solution)/shard_map/average/pallas_call | solution.py:583
  209.0 0.7 copy.41
  209.7 0.6 copy.42
  210.3 0.6 copy.43
  211.0 0.7 copy.44
  (40 shorter events, 0.3 us)
Async XLA Ops:
  0.6 20.4 %copy-start = (bf16[1,2048,512]{2,1,0:T(8,128)(2,1)S(1)}, bf16[1,2048,512]{2,1,0:T(8,128)(2,1)}, u32[]{:S(2)}) copy-start(bf16[1,2048,512]{2,1,0:T(8,128)(2,1)} %param.17) | copy-start | bytes 6291460
  5.6 3.0 %copy-start.6 = (bf16[384,2048]{1,0:T(8,128)(2,1)S(1)}, bf16[384,2048]{1,0:T(8,128)(2,1)}, u32[]{:S(2)}) copy-start(bf16[384,2048]{1,0:T(8,128)(2,1)} %param.12) | copy-start | bytes 4718596
  17.1 1.1 copy-start.10
  17.3 1.9 copy-start.8
  18.2 2.2 %copy-start.4 = (f32[2,384,384,4]{2,1,3,0:T(8,128)}, f32[2,384,384,4]{2,1,3,0:T(8,128)S(1)}, u32[]{:S(2)}) copy-start(f32[2,384,384,4]{2,1,3,0:T(8,128)S(1)} %get-tuple-element.29) | copy-start | bytes 14155780
  19.3 1.2 copy-start.13
  20.4 1.6 copy-start.5
  22.1 42.3 %copy-start.3 = (bf16[1,2048]{1,0:T(2,128)(2,1)S(1)}, bf16[1,2048]{1,0:T(2,128)(2,1)}, u32[]{:S(2)}) copy-start(bf16[1,2048]{1,0:T(2,128)(2,1)} %gain_ref.1) | copy-start | bytes 12292
  113.7 1.2 copy-start.2
  119.8 25.6 %collective-permute-start = (bf16[4,256,512]{2,1,0:T(8,128)(2,1)}, bf16[4,256,512]{2,1,0:T(8,128)(2,1)S(1)}, u32[]{:S(2)}, u32[]{:S(2)}) collective-permute-start(bf16[4,256,512]{2,1,0:T(8,128)(2,1)} %dynamic-slice_bitcast_fusion), channel_id=1, source_target_pairs={{0,1},{1,0},{2,3},{3,2},{4,5},{5,4},{6,7},{7,6},{8,9},{9,8},{10,11... | collective-permute-start | bytes 3145736 | tf_op jit(solution)/shard_map/ppermute | solution.py:573
  126.8 7.0 %slice-start = ((s8[4718592]{0:T(1024)(128)(4,1)}), s8[4194304]{0:T(1024)(128)(4,1)S(1)}, s32[]{:S(2)}) async-start(s8[4718592]{0:T(1024)(128)(4,1)} %bitcast.151), calls=%async_computation | async-start | bytes 8388608
  129.6 4.3 %slice-start.1 = ((s8[4718592]{0:T(1024)(128)(4,1)}), s8[524288]{0:T(1024)(128)(4,1)S(1)}, s32[]{:S(2)}) async-start(s8[4718592]{0:T(1024)(128)(4,1)} %bitcast.151), calls=%async_computation.1 | async-start | bytes 1048576
  129.6 4.3 %copy-start.12 = (pred[384,384]{1,0:T(8,128)(4,1)S(1)}, pred[384,384]{1,0:T(8,128)(4,1)}, u32[]{:S(2)}) copy-start(pred[384,384]{1,0:T(8,128)(4,1)} %iota_compare_fusion) | copy-start | bytes 442372
  133.9 2.2 %copy-start.9 = (bf16[384,8,64]{0,2,1:T(8,128)(2,1)S(1)}, bf16[384,8,64]{0,2,1:T(8,128)(2,1)}, u32[]{:S(2)}) copy-start(bf16[384,8,64]{0,2,1:T(8,128)(2,1)} %copy-done.8) | copy-start | bytes 1179652
  133.9 3.0 %copy-start.11 = (bf16[384,2,64,1]{0,2,3,1:T(8,128)(2,1)S(1)}, bf16[384,2,64,1]{0,2,3,1:T(8,128)(2,1)}, u32[]{:S(2)}) copy-start(bf16[384,2,64,1]{0,2,3,1:T(8,128)(2,1)} %copy-done.10) | copy-start | bytes 294916
  137.4 1.4 copy-start.7
  140.4 5.0 %copy-start.1 = (bf16[2048,512]{1,0:T(8,128)(2,1)S(1)}, bf16[2048,512]{1,0:T(8,128)(2,1)}, u32[]{:S(2)}) copy-start(bf16[2048,512]{1,0:T(8,128)(2,1)} %convolution_convert_fusion.1) | copy-start | bytes 6291460
